TPU v7x, 32 devices: a whole 2x2x4 slice. The times are simulated.
32 devices in a mesh: sub: 16 (over z, y, core), tm: 2 (over x).
Axes of the slice: x: 2, y: 2, z: 4, core: 2. Of those that a mesh axis runs over, the one named last changes fastest.
Arguments:
- voltages: bfloat16 [192, 2, 96, 2048], P('sub', None, None, 'tm'), may hold values from -6 to 6
- pointing_table: bfloat16 [192, 2, 320, 96], P('sub'), may hold values from -0.4375 to 0.4375
- beam_pointing: int32 [256], replicated, may hold values from 0 to 319
- subband_order: int32 [192], replicated, may hold values from 0 to 191, each once
- live_subbands: int32 [1], replicated, may hold values from 152 to 192
- filter_taps: float32 [16, 16], replicated, may hold values from -0.36 to 0.36
Outputs:
- synthesised: bfloat16 [256, 12, 2, 32768], P('sub', None, None, 'tm')
Inputs may be any that keep to these rules, and one draw needn't show every extreme that they name: `subband_order`: each slot is named by exactly one frequency.
All inputs are finite; a program needn't handle non-finite values.
Results may differ from a plain program's by a relative error of at most 0.0052.
Values may be sent and summed in bfloat16 or wider, within the bound.
No kernel may reach another device: no remote copies, remote signals or barrier semaphores. Data moves between devices by JAX's collectives and lax.ppermute only.
A program may use at most 192 MiB of HBM per device.

v0:
```python
import math
import jax
import jax.numpy as jnp
from jax import lax
from jax.sharding import PartitionSpec as P


def shifted(block, axis, distance):
    devices = range(lax.axis_size(axis))
    route = [(i - distance, i) for i in devices if i - distance in devices]
    return lax.ppermute(block, axis, route)


def inverse_table(channel_count):
    channel_index = jnp.arange(channel_count, dtype=jnp.int32)
    phase = (jnp.outer(channel_index, channel_index) % channel_count).astype(jnp.float32) * (
        2.0 * math.pi / channel_count
    )
    cosine = jnp.cos(phase).astype(jnp.bfloat16)
    sine_table = jnp.sin(phase).astype(jnp.bfloat16)
    upper_rows = jnp.stack([cosine, -sine_table], axis=1)
    lower_rows = jnp.stack([sine_table, cosine], axis=1)
    return jnp.stack([upper_rows, lower_rows], axis=0)


def spectrum_channels(beam_rows, subband_order, live_subbands, inverse_rows):
    slot_count = beam_rows.shape[0]
    channel_count = inverse_rows.shape[1]
    spectrum = jnp.take(beam_rows, subband_order, axis=0)
    live_mask = jnp.arange(slot_count, dtype=jnp.int32) < live_subbands[0]
    spectrum = jnp.where(live_mask[:, None, None, None], spectrum, jnp.zeros_like(spectrum))
    grouped = spectrum.reshape(
        slot_count // channel_count, channel_count, beam_rows.shape[1], 2, beam_rows.shape[3]
    )
    channels = jnp.einsum(
        "qkpc,gcbpt->bgqkt", inverse_rows, grouped, preferred_element_type=jnp.float32
    )
    return (grouped, channels)


def polyphase(channels, earlier, filter_taps):
    length = channels.shape[4]
    tap_count = filter_taps.shape[0]
    extended = jnp.concatenate([earlier, channels], axis=4)
    running = jnp.zeros_like(channels)
    for tap_index in range(tap_count):
        offset = tap_count - 1 - tap_index
        running = (
            running + filter_taps[tap_index][:, None] * extended[..., offset : offset + length]
        )
    channel_shape = channels.shape
    return (
        jnp.swapaxes(running, 3, 4)
        .reshape(channel_shape[0], channel_shape[1], 2, length * channel_shape[3])
        .astype(jnp.bfloat16)
    )


def on_device(voltages, pointing_table, beam_pointing, subband_order, live_subbands, filter_taps):
    local_subbands = voltages.shape[0]
    inputs = voltages.shape[2]
    local_time = voltages.shape[3]
    beam_count = beam_pointing.shape[0]
    rim_width = filter_taps.shape[0] - 1
    chosen = jnp.take(pointing_table, beam_pointing, axis=2)
    real_weight = chosen[:, 0]
    imag_weight = chosen[:, 1]
    stacked = jnp.stack(
        [
            jnp.concatenate([real_weight, -imag_weight], axis=2),
            jnp.concatenate([imag_weight, real_weight], axis=2),
        ],
        axis=2,
    )
    stacked = stacked.reshape(local_subbands, 2 * beam_count, 2 * inputs)
    signal = voltages.reshape(local_subbands, 2 * inputs, local_time)
    formed = jnp.einsum("sqi,sit->sqt", stacked, signal, preferred_element_type=jnp.float32).astype(
        jnp.bfloat16
    )
    inverse_rows = inverse_table(filter_taps.shape[1])
    axis_devices = lax.axis_size("sub")
    beam_part = beam_count // axis_devices
    blocks = formed.reshape(local_subbands, axis_devices, beam_part, 2, local_time)
    beam_rows = lax.all_to_all(blocks, "sub", split_axis=1, concat_axis=0, tiled=True)[:, 0]
    grouped, channels = spectrum_channels(beam_rows, subband_order, live_subbands, inverse_rows)
    earlier = shifted(channels[..., local_time - rim_width :].astype(jnp.bfloat16), "tm", 1).astype(
        jnp.float32
    )
    return polyphase(channels, earlier, filter_taps)


def solution(mesh):
    in_specs = (P("sub", None, None, "tm"), P("sub", None, None, None), P(), P(), P(), P())
    out_specs = P("sub", None, None, "tm")
    return jax.shard_map(
        on_device, mesh=mesh, in_specs=in_specs, out_specs=out_specs, check_vma=False
    )
```

profile of v0, /device:TPU:14, one launch (start us, length us, event | category | flops | bytes accessed | tf_op | source)
XLA Modules:
  0.0 792.8 jit_solution(15740473894358660357)
XLA Ops:
  0.0 0.7 compare_and_fusion
  0.7 0.7 compare_select_fusion
  1.4 5.8 copy.47
  7.1 5.2 gather_fusion
  12.4 2.1 fusion.51
  14.5 2.2 fusion.62
  16.7 2.8 copy.49
  19.5 1.1 bitcast_negate_fusion
  20.6 1.3 copy.48
  21.9 1.3 maximum_bitcast_fusion
  23.2 0.2 pad_maximum_fusion.1
  23.4 5.5 copy.50
  28.9 5.2 reshape.129
  34.1 8.9 %convolution_convert_fusion = bf16[12,512,1024]{2,1,0:T(8,128)(2,1)} fusion(bf16[12,512,192]{2,1,0:T(8,128)(2,1)S(1)} %reshape.129, bf16[12,192,1024]{2,1,0:T(8,128)(2,1)} %bitcast.74), kind=kOutput, calls=%fused_computation.81 | convolution fusion | flops 2422210560 | bytes 19660800 | tf_op jit(solution)/shard_map/sqi,sit->sqt/dot_general | solution.py:77
  43.1 19.0 %reshape.131 = bf16[12,16,16,2,1024]{4,3,2,1,0:T(2,128)(2,1)} reshape(bf16[12,512,1024]{2,1,0:T(8,128)(2,1)} %convolution_convert_fusion) | data formatting | bytes 25165824 | tf_op jit(solution)/shard_map/reshape | solution.py:83
  62.1 12.5 %copy.52 = bf16[12,16,16,2,1024]{4,2,3,0,1:T(8,128)(2,1)} copy(bf16[12,16,16,2,1024]{4,3,2,1,0:T(2,128)(2,1)} %reshape.131) | data formatting | bytes 25165824 | tf_op jit(solution)/shard_map/reshape | solution.py:83
  74.6 6.2 all-to-all-start
  81.5 0.1 broadcast_in_dim.41
  81.6 0.1 fusion.60
  81.7 0.1 sine_convert_fusion
  81.8 271.0 %all-to-all-done = bf16[12,16,16,2,1024]{4,2,3,0,1:T(8,128)(2,1)} async-done(((bf16[12,16,16,2,1024]{4,2,3,0,1:T(8,128)(2,1)}), bf16[12,16,16,2,1024]{4,2,3,0,1:T(8,128)(2,1)}, u32[]{:S(2)}, u32[]{:S(2)}) %all-to-all-start) | async-done | bytes 12582944 | tf_op jit(solution)/shard_map/all_to_all | solution.py:84
  352.8 12.8 %gather_fusion.1 = bf16[192,16,2,1024]{3,1,2,0:T(8,128)(2,1)} fusion(bf16[192,16,2,1024]{3,1,2,0:T(8,128)(2,1)} %bitcast.10, s32[1024]{0:T(1024)S(1)} %pad_clamp_fusion), kind=kCustom, calls=%fused_computation.1 | custom fusion | bytes 25166592 | tf_op jit(solution)/shard_map/jit(_take)/gather | solution.py:29
  365.6 6.8 select_bitcast_fusion
  372.4 12.4 %fusion.48 = f32[16,12,2,16,1024]{4,3,2,0,1:T(8,128)} fusion(bf16[12,16,16,2,1024,1]{4,2,3,1,0,5:T(8,128)(2,1)S(1)} %select_bitcast_fusion, bf16[1,16,2,16]{3,1,2,0:T(8,128)(2,1)S(1)} %get-tuple-element.26, bf16[1,16,2,16]{3,1,2,0:T(8,128)(2,1)S(1)} %get-tuple-element.25), kind=kOutput, calls=%fused_computation.80 | convolution fusion | flops 402657280 | bytes 37750784 | tf_op jit(solution)/shard_map/qkpc,gcbpt->bgqkt/dot_general | solution.py:35
  384.8 2.4 slice.415
  387.2 3.1 copy.54
  390.3 1.5 collective-permute-start
  391.8 35.0 %collective-permute-done = bf16[16,12,2,16,15]{3,0,4,2,1:T(8,128)(2,1)} collective-permute-done((bf16[16,12,2,16,15]{3,0,4,2,1:T(8,128)(2,1)S(1)}, bf16[16,12,2,16,15]{3,0,4,2,1:T(8,128)(2,1)}, u32[]{:S(2)}, u32[]{:S(2)}) %collective-permute-start) | collective-permute-done | bytes 184352 | tf_op jit(solution)/shard_map/ppermute | solution.py:11
  426.9 3.5 copy.55
  430.4 168.7 %fusion.47 = bf16[16,12,2,1024,16]{3,4,2,0,1:T(8,128)(2,1)} fusion(f32[16,12,2,16,1024]{4,3,2,0,1:T(8,128)} %fusion.48, f32[16,12,2,16,15]{4,3,2,0,1:T(8,128)S(1)} %copy.55, f32[16]{0:T(128)S(1)} %get-tuple-element.23, f32[16]{0:T(128)S(1)} %get-tuple-element.24, f32[16]{0:T(128)S(1)} %get-tuple-element.10, f32[16]{0:T(128)S(1)} %get-tuple-element.11, ...), kind=kLoop, calls=%fused_computation.79 | loop fusion | flops 295698432 | bytes 38118400 | tf_op jit(solution)/shard_map/convert_element_type | solution.py:55
  599.1 77.5 %copy.64 = bf16[16,12,2,1024,16]{4,3,2,1,0:T(8,128)(2,1)} copy(bf16[16,12,2,1024,16]{3,4,2,0,1:T(8,128)(2,1)} %fusion.47) | data formatting | bytes 25165824 | tf_op jit(solution)/shard_map/convert_element_type | solution.py:55
  676.7 116.1 %reshape.153 = bf16[16,12,2,16384]{3,2,1,0:T(2,128)(2,1)} reshape(bf16[16,12,2,1024,16]{4,3,2,1,0:T(8,128)(2,1)} %copy.64) | data formatting | bytes 25165824 | tf_op jit(solution)/shard_map/convert_element_type | solution.py:55
  (11 shorter events, 0.1 us)
Async XLA Ops:
  62.1 19.4 %copy-start.1 = (s32[192]{0:T(256)S(1)}, s32[192]{0:T(256)}, u32[]{:S(2)}) copy-start(s32[192]{0:T(256)} %param.9) | copy-start | bytes 2308
  74.6 278.2 %all-to-all-start = ((bf16[12,16,16,2,1024]{4,2,3,0,1:T(8,128)(2,1)}), bf16[12,16,16,2,1024]{4,2,3,0,1:T(8,128)(2,1)}, u32[]{:S(2)}, u32[]{:S(2)}) async-start(bf16[12,16,16,2,1024]{4,2,3,0,1:T(8,128)(2,1)} %copy.52), calls=%async_computation | async-start | bytes 25165824 | tf_op jit(solution)/shard_map/all_to_all | solution.py:84
  372.4 19.4 %copy-start = (f32[16,16]{1,0:T(8,128)S(1)}, f32[16,16]{1,0:T(8,128)}, u32[]{:S(2)}) copy-start(f32[16,16]{1,0:T(8,128)} %param.11) | copy-start | bytes 3076
  390.3 36.6 %collective-permute-start = (bf16[16,12,2,16,15]{3,0,4,2,1:T(8,128)(2,1)S(1)}, bf16[16,12,2,16,15]{3,0,4,2,1:T(8,128)(2,1)}, u32[]{:S(2)}, u32[]{:S(2)}) collective-permute-start(bf16[16,12,2,16,15]{3,0,4,2,1:T(8,128)(2,1)S(1)} %copy.54), channel_id=1, source_target_pairs={{0,1},{2,3},{4,5},{6,7},{8,9},{10,11},{12,13},{14,15},{16,17},{18,... | collective-permute-start | bytes 552968 | tf_op jit(solution)/shard_map/ppermute | solution.py:11
where the time goes:
time: 799 us; the launch traced here: 793 us
  waiting for transfers between devices  306 us (38%)
  local copies, waits for them, and re-layouts  275 us (34%)
  other arithmetic  182 us (23%)
  matrix products  21.3 us (3%)
    all_to_all x1, waiting for transfers between devices, on_device(): lax.all_to_all(blocks, 'sub', split_axis=1, concat_axis=0, tiled=True)[:, 0]  271 us
    convert_element_type x2, local copies, waits for them, and re-layouts, polyphase(): return jnp.swapaxes(running, 3, 4).reshape(channel_shape[0], channel_shap...  194 us
    convert_element_type x1, other arithmetic, polyphase(): return jnp.swapaxes(running, 3, 4).reshape(channel_shape[0], channel_shap...  169 us
    ppermute x1, waiting for transfers between devices, shifted(): return lax.ppermute(block, axis, route)  35 us
    reshape x2, local copies, waits for them, and re-layouts, on_device(): formed.reshape(local_subbands, axis_devices, beam_part, 2, local_time)  31.6 us
  transfers between devices with their start and end apart: 2, of which 2 were waited for; matrix products, arithmetic and copies ran while one was open for 0% of the time, Pallas kernels for 0%

commit v1 on v0

--- a/solution.py
+++ b/solution.py
@@ -81,7 +81,15 @@
     axis_devices = lax.axis_size("sub")
     beam_part = beam_count // axis_devices
     blocks = formed.reshape(local_subbands, axis_devices, beam_part, 2, local_time)
-    beam_rows = lax.all_to_all(blocks, "sub", split_axis=1, concat_axis=0, tiled=True)[:, 0]
+    beam_rows = jnp.concatenate(
+        lax.all_to_all(
+            jnp.stack(jnp.split(blocks, lax.axis_size("sub"), 1), axis=0),
+            split_axis=0,
+            axis_name="sub",
+            concat_axis=0,
+        ),
+        0,
+    )[:, 0]
     grouped, channels = spectrum_channels(beam_rows, subband_order, live_subbands, inverse_rows)
     earlier = shifted(channels[..., local_time - rim_width :].astype(jnp.bfloat16), "tm", 1).astype(
         jnp.float32

time: 799 us -> 842 us (1.054)
  local copies, waits for them, and re-layouts: 275 us -> 318 us
    unnamed x5 -> x20, local copies, waits for them, and re-layouts: 5.77 us -> 45.8 us
    reshape x2 -> x1, local copies, waits for them, and re-layouts: 31.6 us -> 19 us  [on_device(): formed.reshape(local_subbands, axis_devices, beam_part, 2, local_time)]
    all_to_all x0 -> x1, local copies, waits for them, and re-layouts: none -> 12.5 us  [on_device(): lax.all_to_all(jnp.stack(jnp.split(blocks, lax.axis_size('sub'), 1), axis...]
where the time goes in v1:
time: 842 us; the launch traced here: 836 us
  local copies, waits for them, and re-layouts  318 us (38%)
  waiting for transfers between devices  306 us (36%)
  other arithmetic  182 us (22%)
  matrix products  21.3 us (3%)
    all_to_all x1, waiting for transfers between devices, on_device(): lax.all_to_all(jnp.stack(jnp.split(blocks, lax.axis_size('sub'), 1), axis...  271 us
    convert_element_type x2, local copies, waits for them, and re-layouts, polyphase(): return jnp.swapaxes(running, 3, 4).reshape(channel_shape[0], channel_shap...  194 us
    convert_element_type x1, other arithmetic, polyphase(): return jnp.swapaxes(running, 3, 4).reshape(channel_shape[0], channel_shap...  169 us
    unnamed x20, local copies, waits for them, and re-layouts  45.8 us
    ppermute x1, waiting for transfers between devices, shifted(): return lax.ppermute(block, axis, route)  35.3 us
    reshape x1, local copies, waits for them, and re-layouts, on_device(): formed.reshape(local_subbands, axis_devices, beam_part, 2, local_time)  19 us
  transfers between devices with their start and end apart: 2, of which 2 were waited for; matrix products, arithmetic and copies ran while one was open for 0% of the time, Pallas kernels for 0%

profile of v1, /device:TPU:14, one launch (start us, length us, event | category | flops | bytes accessed | tf_op | source)
XLA Modules:
  0.0 835.6 jit_solution(8149960359821808907)
XLA Ops:
  1.4 5.8 copy.121
  7.1 5.2 gather_fusion
  16.7 2.8 copy.123
  23.4 5.5 copy.124
  28.9 5.2 reshape.128
  34.1 8.9 %convolution_convert_fusion = bf16[12,512,1024]{2,1,0:T(8,128)(2,1)} fusion(bf16[12,512,192]{2,1,0:T(8,128)(2,1)S(1)} %reshape.128, bf16[12,192,1024]{2,1,0:T(8,128)(2,1)} %bitcast.165), kind=kOutput, calls=%fused_computation.81 | convolution fusion | flops 2422210560 | bytes 19660800 | tf_op jit(solution)/shard_map/sqi,sit->sqt/dot_general | solution.py:77
  43.1 19.0 %reshape.130 = bf16[12,16,16,2,1024]{4,3,2,1,0:T(2,128)(2,1)} reshape(bf16[12,512,1024]{2,1,0:T(8,128)(2,1)} %convolution_convert_fusion) | data formatting | bytes 25165824 | tf_op jit(solution)/shard_map/reshape | solution.py:83
  62.1 2.7 fusion.67
  64.8 2.7 fusion.66
  67.4 2.7 fusion.65
  70.1 2.7 fusion.64
  72.8 2.7 fusion.63
  75.4 2.7 fusion.62
  78.1 2.7 fusion.61
  80.8 2.7 fusion.60
  83.5 2.7 fusion.59
  86.1 2.7 fusion.58
  88.8 2.7 fusion.57
  94.1 2.7 fusion.55
  102.1 2.7 fusion.52
  104.8 6.4 all-to-all-start
  112.1 271.0 %all-to-all-done = bf16[16,12,1,16,2,1024]{5,4,3,1,2,0:T(2,128)(2,1)} async-done(((bf16[16,12,1,16,2,1024]{5,4,3,1,2,0:T(2,128)(2,1)}), bf16[16,12,1,16,2,1024]{5,4,3,1,2,0:T(2,128)(2,1)}, u32[]{:S(2)}, u32[]{:S(2)}) %all-to-all-start) | async-done | bytes 12582944 | tf_op jit(solution)/shard_map/all_to_all | solution.py:85
  383.1 12.5 %copy.141 = bf16[16,12,1,16,2,1024]{5,3,4,1,0,2:T(8,128)(2,1)} copy(bf16[16,12,1,16,2,1024]{5,4,3,1,2,0:T(2,128)(2,1)} %all-to-all-done) | data formatting | bytes 25165824 | tf_op jit(solution)/shard_map/all_to_all | solution.py:85
  395.7 12.8 %gather_fusion.1 = bf16[192,16,2,1024]{3,1,2,0:T(8,128)(2,1)} fusion(bf16[192,16,2,1024]{3,1,2,0:T(8,128)(2,1)} %bitcast.162, s32[1024]{0:T(1024)S(1)} %pad_clamp_fusion), kind=kCustom, calls=%fused_computation.1 | custom fusion | bytes 25166592 | tf_op jit(solution)/shard_map/jit(_take)/gather | solution.py:29
  408.5 6.8 select_bitcast_fusion
  415.3 12.4 %fusion.48 = f32[16,12,2,16,1024]{4,3,2,0,1:T(8,128)} fusion(bf16[12,16,16,2,1024,1]{4,2,3,1,0,5:T(8,128)(2,1)S(1)} %select_bitcast_fusion, bf16[1,16,2,16]{3,1,2,0:T(8,128)(2,1)S(1)} %get-tuple-element.26, bf16[1,16,2,16]{3,1,2,0:T(8,128)(2,1)S(1)} %get-tuple-element.25), kind=kOutput, calls=%fused_computation.80 | convolution fusion | flops 402657280 | bytes 37750784 | tf_op jit(solution)/shard_map/qkpc,gcbpt->bgqkt/dot_general | solution.py:35
  430.0 3.1 copy.143
  434.5 35.3 %collective-permute-done = bf16[16,12,2,16,15]{3,0,4,2,1:T(8,128)(2,1)} collective-permute-done((bf16[16,12,2,16,15]{3,0,4,2,1:T(8,128)(2,1)S(1)}, bf16[16,12,2,16,15]{3,0,4,2,1:T(8,128)(2,1)}, u32[]{:S(2)}, u32[]{:S(2)}) %collective-permute-start) | collective-permute-done | bytes 184352 | tf_op jit(solution)/shard_map/ppermute | solution.py:11
  469.7 3.5 copy.144
  473.3 168.7 %fusion.47 = bf16[16,12,2,1024,16]{3,4,2,0,1:T(8,128)(2,1)} fusion(f32[16,12,2,16,1024]{4,3,2,0,1:T(8,128)} %fusion.48, f32[16,12,2,16,15]{4,3,2,0,1:T(8,128)S(1)} %copy.144, f32[16]{0:T(128)S(1)} %get-tuple-element.23, f32[16]{0:T(128)S(1)} %get-tuple-element.24, f32[16]{0:T(128)S(1)} %get-tuple-element.10, f32[16]{0:T(128)S(1)} %get-tuple-element.11, ...), kind=kLoop, calls=%fused_computation.79 | loop fusion | flops 295698432 | bytes 38118400 | tf_op jit(solution)/shard_map/convert_element_type | solution.py:55
  642.0 77.5 %copy.153 = bf16[16,12,2,1024,16]{4,3,2,1,0:T(8,128)(2,1)} copy(bf16[16,12,2,1024,16]{3,4,2,0,1:T(8,128)(2,1)} %fusion.47) | data formatting | bytes 25165824 | tf_op jit(solution)/shard_map/convert_element_type | solution.py:55
  719.5 116.1 %reshape.152 = bf16[16,12,2,16384]{3,2,1,0:T(2,128)(2,1)} reshape(bf16[16,12,2,1024,16]{4,3,2,1,0:T(8,128)(2,1)} %copy.153) | data formatting | bytes 25165824 | tf_op jit(solution)/shard_map/convert_element_type | solution.py:55
  (27 shorter events, 21.6 us)
Async XLA Ops:
  104.8 7.0 copy-start.1
  104.8 278.3 %all-to-all-start = ((bf16[16,12,1,16,2,1024]{5,4,3,1,2,0:T(2,128)(2,1)}), bf16[16,12,1,16,2,1024]{5,4,3,1,2,0:T(2,128)(2,1)}, u32[]{:S(2)}, u32[]{:S(2)}) async-start(bf16[16,12,1,16,2,1024]{5,4,3,1,2,0:T(2,128)(2,1)} %fusion.52), calls=%async_computation | async-start | bytes 25165824 | tf_op jit(solution)/shard_map/all_to_all | solution.py:85
  415.2 19.2 %copy-start = (f32[16,16]{1,0:T(8,128)S(1)}, f32[16,16]{1,0:T(8,128)}, u32[]{:S(2)}) copy-start(f32[16,16]{1,0:T(8,128)} %param.11) | copy-start | bytes 3076
  433.1 36.6 %collective-permute-start = (bf16[16,12,2,16,15]{3,0,4,2,1:T(8,128)(2,1)S(1)}, bf16[16,12,2,16,15]{3,0,4,2,1:T(8,128)(2,1)}, u32[]{:S(2)}, u32[]{:S(2)}) collective-permute-start(bf16[16,12,2,16,15]{3,0,4,2,1:T(8,128)(2,1)S(1)} %copy.143), channel_id=1, source_target_pairs={{0,1},{2,3},{4,5},{6,7},{8,9},{10,11},{12,13},{14,15},{16,17},{18,... | collective-permute-start | bytes 552968 | tf_op jit(solution)/shard_map/ppermute | solution.py:11
